TPU v7x, 32 devices: a whole 2x2x4 slice. The times are simulated.
32 devices in a mesh: fsdp: 4 (over y, x), head: 4 (over z), tensor: 2 (over core).
Axes of the slice: x: 2, y: 2, z: 4, core: 2. Of those that a mesh axis runs over, the one named last changes fastest.
Arguments:
- activations: bfloat16 [2, 16, 197, 768], P(None, ('fsdp', 'head')), may hold values from -6 to 6
- w_qkv: bfloat16 [3, 768, 768], P(None, 'fsdp', 'head'), may hold values from -0.21875 to 0.21875
- w_out: bfloat16 [768, 768], P('head', 'fsdp'), may hold values from -0.875 to 0.875
- gain_one: float32 [768], replicated, may hold values from 0.5 to 1.5
- gain_two: float32 [768], replicated, may hold values from 0.5 to 1.5
- w_router: bfloat16 [768, 8], replicated, may hold values from -0.15625 to 0.15625
- w_in: bfloat16 [8, 768, 3072], P('head', 'fsdp', 'tensor'), may hold values from -0.21875 to 0.21875
- w_down: bfloat16 [8, 3072, 768], P('head', 'tensor', 'fsdp'), may hold values from -0.625 to 0.625
- routes: int32 [2, 16, 197, 2], P(None, ('fsdp', 'head')), may hold values from 0 to 7, as said below
- slot_index: int32 [2, 16, 197, 2], P(None, ('fsdp', 'head')), may hold values from 0 to 63, as said below
- keep_mask: int32 [2, 16, 197, 2], P(None, ('fsdp', 'head')), may hold values from 0 to 1, as said below
- cotangent: bfloat16 [2, 16, 197, 768], P(None, ('fsdp', 'head')), may hold values from -6 to 6
Outputs:
- block_out: bfloat16 [2, 16, 197, 768], P(None, ('fsdp', 'head'))
- grad_input: float32 [2, 16, 197, 768], P(None, ('fsdp', 'head'))
- grad_qkv: float32 [3, 768, 768], P(None, 'fsdp', 'head')
- grad_out: float32 [768, 768], P('head', 'fsdp')
- grad_gain_one: float32 [768], replicated
- grad_gain_two: float32 [768], replicated
- grad_router: float32 [768, 8], replicated
- grad_in: float32 [8, 768, 3072], P('head', 'fsdp', 'tensor')
- grad_down: float32 [8, 3072, 768], P('head', 'tensor', 'fsdp')
Inputs may be any that keep to these rules, and one draw needn't show every extreme that they name: `routes`: the 2 experts of a token differ. In every micro-batch and for every index of fsdp there is an expert that 72 or more rows of each device along head name. `slot_index`: among the kept pairs of one device's rows of one micro-batch that name one expert, slots are distinct. `keep_mask`: of one device's rows of one micro-batch, at most 64 pairs naming one expert are kept, and a pair is dropped only where 64 pairs of that expert are kept; in every micro-batch and index of fsdp some expert has exactly 64 kept pairs from each device along head.
All inputs are finite; a program needn't handle non-finite values.
Results may differ from a plain program's by a relative error of at most 0.02.
Values may be sent and summed in bfloat16 or wider, within the bound.
A program may use at most 192 MiB of HBM per device.

v0:
```python
import jax
import jax.numpy as jnp
from jax import lax
from jax.sharding import PartitionSpec as P

HD = 64
TOP = 2
CAP = 64
highest = lax.Precision.HIGHEST
norm_eps = 1e-06
f32 = jnp.float32
bf16 = jnp.bfloat16


def norm_rows(values, gain_vec):
    centre = values - jnp.mean(values, axis=-1, keepdims=True)
    spread = jnp.mean(centre * centre, axis=-1, keepdims=True)
    return centre * lax.rsqrt(spread + norm_eps) * gain_vec


def gelu_exact(values):
    return jax.nn.gelu(values, approximate=False)


def softmax_last(values):
    return jax.nn.softmax(values, axis=-1)


def ein(spec, left, right):
    return jnp.einsum(spec, left, right, preferred_element_type=f32)


def swap(values):
    return lax.ppermute(values, "tensor", ((0, 1), (1, 0)))


def pick(values):
    return lax.dynamic_index_in_dim(values, lax.axis_index("tensor"), 0, keepdims=False)


def both(mine):
    other = swap(mine)
    first = lax.axis_index("tensor") == 0
    return jnp.stack([jnp.where(first, mine, other), jnp.where(first, other, mine)])


def on_device(
    activations,
    w_qkv,
    w_out,
    gain_one,
    gain_two,
    w_router,
    w_in,
    w_down,
    routes,
    slot_index,
    keep_mask,
    cotangent,
):
    _, img_count, seq_length, width = activations.shape
    groups = lax.axis_size("head")
    local_heads = w_qkv.shape[2] // HD
    local_experts = w_in.shape[0]
    total_experts = local_experts * groups
    slot_count = total_experts * CAP
    tok_rows = img_count * seq_length
    head_scale = HD ** (-0.5)
    qkv_full = lax.all_gather(w_qkv, "fsdp", axis=1, tiled=True)
    out_full = lax.all_gather(w_out, "fsdp", axis=1, tiled=True)
    inputs = pick(activations).astype(f32)
    upstream = pick(cotangent).astype(f32).reshape(tok_rows, width)
    route_rows = pick(routes).reshape(tok_rows, TOP)
    slot_rows = pick(slot_index).reshape(tok_rows, TOP)
    keep_int = pick(keep_mask).reshape(tok_rows, TOP)
    normed, norm_back_one = jax.vjp(norm_rows, inputs, gain_one)
    rows_all = lax.all_gather(normed.astype(bf16), "head", axis=0, tiled=True)
    in_full = lax.all_gather(w_in, "fsdp", axis=1, tiled=True)
    down_full = lax.all_gather(w_down, "fsdp", axis=2, tiled=True)
    image_total = rows_all.shape[0]
    head_shape = (image_total, seq_length, local_heads, HD)
    project = ein("bsd,pde->pbse", rows_all, qkv_full)
    queries = (project[0] * head_scale).astype(bf16).reshape(head_shape)
    key_rows = project[1].astype(bf16).reshape(head_shape)
    value_rows = project[2].astype(bf16).reshape(head_shape)
    scores = ein("bqhd,bkhd->bhqk", queries, key_rows)
    top_score = jnp.max(scores, axis=-1, keepdims=True)
    expo_scores = jnp.exp(scores - top_score)
    row_total = jnp.sum(expo_scores, axis=-1, keepdims=True)
    attn_full = expo_scores / row_total
    attn_low = attn_full.astype(bf16)
    mixed_heads = ein("bhqk,bkhd->bqhd", attn_low, value_rows)
    mixed_heads = mixed_heads.reshape(image_total, seq_length, local_heads * HD).astype(bf16)
    partial_att = ein("bsc,cd->bsd", mixed_heads, out_full)
    attended = lax.psum_scatter(
        partial_att.astype(bf16), "head", scatter_dimension=0, tiled=True
    ).astype(f32)
    hidden = inputs + attended
    normed_two, norm_back_two = jax.vjp(norm_rows, hidden, gain_two)
    token_low = normed_two.astype(bf16).reshape(tok_rows, width)
    logits = jnp.dot(token_low, w_router, preferred_element_type=f32)
    gate_probs, softmax_back = jax.vjp(softmax_last, logits)
    keep_rows = keep_int.astype(f32)
    expert_ids = jnp.arange(total_experts, dtype=jnp.int32)
    slot_ids = jnp.arange(slot_count, dtype=jnp.int32)
    chosen = (route_rows[:, :, None] == expert_ids[None, None, :]).astype(f32)
    gate_values = jnp.sum(gate_probs[:, None, :] * chosen, axis=2) * keep_rows
    flat_slot = route_rows * CAP + slot_rows
    onehot = (
        (flat_slot.T[:, :, None] == slot_ids[None, None, :]) & (keep_int.T[:, :, None] == 1)
    ).astype(bf16)
    weighted = (gate_values.T[:, :, None] * upstream[None, :, :]).astype(bf16)
    tokens_two = jnp.broadcast_to(token_low[None], weighted.shape)
    sent = ein("ktc,ktd->cd", onehot, jnp.concatenate([tokens_two, weighted], axis=-1))
    sent = sent.astype(bf16).reshape(groups, local_experts, CAP, 2 * width)
    mine = lax.all_to_all(sent, "head", split_axis=0, concat_axis=0, tiled=True)
    slots = jnp.stack([mine, swap(mine)])
    received = slots[..., :width]
    slot_grad = slots[..., width:]
    up_proj = ein("mgecd,edf->emgcf", received, in_full)
    active, gelu_back = jax.vjp(gelu_exact, up_proj)
    active = active.astype(bf16)
    partial_out = ein("emgcf,efd->mgecd", active, down_full)
    active_grad = ein("mgecd,efd->emgcf", slot_grad, down_full)
    up_grad = gelu_back(active_grad)[0].astype(bf16)
    partial_in = ein("emgcf,edf->mgecd", up_grad, in_full)
    grad_down = ein("emgcf,mgecd->efd", active, slot_grad)
    grad_in = ein("mgecd,emgcf->edf", received, up_grad)
    partial = jnp.concatenate([partial_out, partial_in], axis=-1)
    back = (partial[0] + swap(partial[1].astype(bf16)).astype(f32)).astype(bf16)
    back = lax.all_to_all(back, "head", split_axis=0, concat_axis=0, tiled=True)
    back = back.reshape(slot_count, 2 * width)
    picked_two = ein("ktc,cd->ktd", onehot, back)
    picked = picked_two[..., :width]
    token_grad = picked_two[0, :, width:] + picked_two[1, :, width:]
    moe_out = jnp.sum(gate_values.T[:, :, None] * picked, axis=0)
    block_out = (hidden + moe_out.reshape(img_count, seq_length, width)).astype(bf16)
    gate_grad = jnp.sum(upstream[None] * picked, axis=-1).T * keep_rows
    prob_grad = jnp.sum(gate_grad[:, :, None] * chosen, axis=1)
    logit_grad = softmax_back(prob_grad)[0]
    grad_router = jnp.dot(token_low.astype(f32).T, logit_grad, precision=highest)
    token_grad = token_grad + jnp.dot(logit_grad, w_router.astype(f32).T, precision=highest)
    hidden_part, grad_gain_two = norm_back_two(token_grad.reshape(img_count, seq_length, width))
    hidden_grad = upstream.reshape(img_count, seq_length, width) + hidden_part
    att_grad_all = lax.all_gather(hidden_grad.astype(bf16), "head", axis=0, tiled=True)
    grad_out = ein("bsc,bsd->cd", mixed_heads, att_grad_all)
    mixed_grad = ein("bsd,cd->bsc", att_grad_all, out_full).astype(bf16).reshape(head_shape)
    value_grad = ein("bhqk,bqhd->bkhd", attn_low, mixed_grad).astype(bf16)
    prob_grads = ein("bqhd,bkhd->bhqk", mixed_grad, value_rows)
    row_delta = jnp.sum(prob_grads * attn_full, axis=-1, keepdims=True)
    score_grad = (attn_full * (prob_grads - row_delta)).astype(bf16)
    query_grad = (ein("bhqk,bkhd->bqhd", score_grad, key_rows) * head_scale).astype(bf16)
    key_grad = ein("bhqk,bqhd->bkhd", score_grad, queries).astype(bf16)
    proj_grad = jnp.stack([query_grad, key_grad, value_grad]).reshape(
        3, image_total, seq_length, local_heads * HD
    )
    row_part = ein("pbse,pde->bsd", proj_grad, qkv_full)
    row_grad = lax.psum_scatter(
        row_part.astype(bf16), "head", scatter_dimension=0, tiled=True
    ).astype(f32)
    grad_qkv = ein("bsd,pbse->pde", rows_all, proj_grad)
    input_part, grad_gain_one = norm_back_one(row_grad)
    input_grad = hidden_grad + input_part

    def owner(part, dim):
        part = lax.psum_scatter(part.astype(bf16), "fsdp", scatter_dimension=dim, tiled=True)
        return part

    def owner_two(part, dim):
        part = owner(part, dim)
        return part.astype(f32) + swap(part).astype(f32)

    small = lax.psum((grad_gain_one, grad_gain_two, grad_router), ("fsdp", "head", "tensor"))
    return (
        both(block_out),
        both(input_grad),
        owner_two(grad_qkv, 1),
        owner_two(grad_out, 1),
        *small,
        owner(grad_in, 1).astype(f32),
        owner(grad_down, 2).astype(f32),
    )


def solution(mesh):
    rows = P(None, ("fsdp", "head"), None, None)
    in_specs = (
        rows,
        P(None, "fsdp", "head"),
        P("head", "fsdp"),
        P(),
        P(),
        P(),
        P("head", "fsdp", "tensor"),
        P("head", "tensor", "fsdp"),
        rows,
        rows,
        rows,
        rows,
    )
    out_specs = (
        rows,
        rows,
        P(None, "fsdp", "head"),
        P("head", "fsdp"),
        P(),
        P(),
        P(),
        P("head", "fsdp", "tensor"),
        P("head", "tensor", "fsdp"),
    )
    return jax.shard_map(
        on_device, mesh=mesh, in_specs=in_specs, out_specs=out_specs, check_vma=False
    )
```

profile of v0, /device:TPU:0, one launch (start us, length us, event | category | flops | bytes accessed | tf_op | source)
XLA Modules:
  0.0 518.0 jit_solution(9751888236601514068)
XLA Ops:
  12.1 19.2 %all_gather.19 = bf16[3,768,192]{2,0,1:T(4,128)(2,1)S(1)} all-gather(bf16[3,192,192]{2,0,1:T(4,128)(2,1)S(1)} %copy.105), channel_id=1, replica_groups=mesh['fsdp'=4,'head'=4,'tensor'=2] {'fsdp'}, dimensions={1}, use_global_device_ids=true | all-gather | bytes 1105920 | tf_op jit(solution)/shard_map/all_gather | solution.py:69
  32.3 10.4 %all_gather.20 = bf16[192,768]{0,1:T(8,128)(2,1)} all-gather(bf16[192,192]{0,1:T(8,128)(2,1)S(1)} %copy.108), channel_id=1, replica_groups=mesh['fsdp'=4,'head'=4,'tensor'=2] {'fsdp'}, dimensions={1}, use_global_device_ids=true | all-gather | bytes 368640 | tf_op jit(solution)/shard_map/all_gather | solution.py:70
  42.7 3.0 all-gather.5.cloned.1.call-done
  59.4 25.5 %reduce-scatter.11.cloned.1.call-done = bf16[1,197,768]{2,1,0:T(8,128)(2,1)} async-done(((bf16[4,197,768]{2,1,0:T(8,128)(2,1)}), bf16[1,197,768]{2,1,0:T(8,128)(2,1)}) %reduce-scatter.11.cloned.1.call-update) | async-done | bytes 302608 | tf_op jit(solution)/shard_map/reduce_scatter | solution.py:95
  91.2 39.7 %all_to_all.10 = bf16[4,2,64,1536]{3,2,1,0:T(8,128)(2,1)S(1)} all-to-all(bf16[4,2,64,1536]{3,2,1,0:T(8,128)(2,1)S(1)} %bitcast.259), channel_id=1, replica_groups=mesh['fsdp'=4,'head'=4,'tensor'=2] {'head'}, dimensions={0} | all-to-all | bytes 3145728 | tf_op jit(solution)/shard_map/all_to_all | solution.py:116
  132.2 3.7 collective-permute-done
  135.9 3.9 pad_maximum_fusion.1
  139.9 7.0 %fusion.33 = (u8[2,2,64,1536]{3,2,1,0:T(8,128)(4,1)S(1)}, u8[2,2,64,1536]{3,2,1,0:T(8,128)(4,1)S(1)}, f32[2,2,4,64,1536]{4,3,2,1,0:T(8,128)S(1)}) fusion(bf16[2,4,2,64,768]{4,3,1,0,2:T(8,128)(2,1)} %get-tuple-element.63, bf16[2,768,1536]{2,1,0:T(8,128)(2,1)} %all-gather.7.cloned.1.call-done), kind=kOutput, calls=%fused_computation.59 | convolution fusion | flops 2435579904 | bytes 13369344 | tf_op jit(solution)/shard_map/mgecd,edf->emgcf/dot_general | solution.py:30
  149.5 15.2 %multiply_convert_fusion = (bf16[2,2,4,64,1536]{4,3,2,1,0:T(8,128)(2,1)}, f32[2,2,4,64,1536]{4,3,2,1,0:T(8,128)}) fusion(f32[2,2,4,64,1536]{4,3,2,1,0:T(8,128)S(1)} %get-tuple-element.79, u8[2,2,64,1536]{3,2,1,0:T(8,128)(4,1)S(1)} %get-tuple-element.46, u8[2,2,64,1536]{3,2,1,0:T(8,128)(4,1)S(1)} %get-tuple-element.45), kind=kLoop, calls=%fused_computation.13 | loop fusion | flops 110100480 | bytes 16515072 | tf_op jit(solution)/shard_map/convert_element_type | solution.py:122
  164.7 23.6 %all-gather.9.cloned.1.call-done = bf16[2,1536,768]{1,2,0:T(8,128)(2,1)} async-done(((bf16[2,1536,192]{1,2,0:T(8,128)(2,1)}), bf16[2,1536,768]{1,2,0:T(8,128)(2,1)}) %all-gather.9.cloned.1.call-update) | async-done | bytes 4718608 | tf_op jit(solution)/shard_map/all_gather | solution.py:79
  188.3 10.4 %add_convert_fusion = bf16[2,2,4,64,1536]{4,3,2,1,0:T(8,128)(2,1)S(1)} fusion(f32[2,2,4,64,1536]{4,3,2,1,0:T(8,128)} %get-tuple-element.59, bf16[2,4,2,64,768]{4,3,1,0,2:T(8,128)(2,1)} %get-tuple-element.62, f32[2,2,4,64,1536]{4,3,2,1,0:T(8,128)} %copy-done.8, bf16[2,1536,768]{1,2,0:T(8,128)(2,1)} %all-gather.9.cloned.1.call-done), kind=kOutput, calls=%fused_computation.12 | convolution fusion | flops 2437939200 | bytes 22020096 | tf_op jit(solution)/shard_map/mgecd,efd->emgcf/dot_general | solution.py:30
  198.7 5.7 %fusion.25 = f32[2,4,2,64,768]{4,3,1,0,2:T(8,128)S(1)} fusion(bf16[2,2,4,64,1536]{4,3,2,1,0:T(8,128)(2,1)S(1)} %add_convert_fusion, bf16[2,768,1536]{2,1,0:T(8,128)(2,1)} %all-gather.7.cloned.1.call-done), kind=kOutput, calls=%fused_computation.50 | convolution fusion | flops 2415919104 | bytes 11010048 | tf_op jit(solution)/shard_map/emgcf,edf->mgecd/dot_general | solution.py:30
  207.4 3.4 collective-permute-done.1
  212.5 4.6 all-to-all-start.1
  217.3 37.2 %all-to-all-done.1 = bf16[4,2,64,1536]{3,2,1,0:T(8,128)(2,1)} async-done(((bf16[4,2,64,1536]{3,2,1,0:T(8,128)(2,1)}), bf16[4,2,64,1536]{3,2,1,0:T(8,128)(2,1)}, u32[]{:S(2)}, u32[]{:S(2)}) %all-to-all-start.1) | async-done | bytes 1572896 | tf_op jit(solution)/shard_map/all_to_all | solution.py:131
  262.0 29.3 %all-gather.11.cloned.1.call-done = bf16[4,197,768]{2,1,0:T(8,128)(2,1)} async-done(((bf16[1,197,768]{2,1,0:T(8,128)(2,1)}), bf16[4,197,768]{2,1,0:T(8,128)(2,1)}) %all-gather.11.cloned.1.call-update) | async-done | bytes 1210384 | tf_op jit(solution)/shard_map/all_gather | solution.py:145
  303.3 3.5 bitcast_convert_fusion.2
  313.0 7.2 %bitcast_convert_fusion.1 = bf16[2,768,1536]{2,1,0:T(8,128)(2,1)} fusion(bf16[2,2,4,64,1536]{4,3,2,1,0:T(8,128)(2,1)} %copy-done.35, bf16[2,4,2,64,768]{4,3,1,0,2:T(8,128)(2,1)} %get-tuple-element.63), kind=kOutput, calls=%fused_computation.3 | convolution fusion | flops 2418278400 | bytes 9437184 | tf_op jit(solution)/shard_map/mgecd,emgcf->edf/dot_general | solution.py:30
  321.6 6.3 %bitcast_convert_fusion = bf16[2,1536,768]{1,2,0:T(8,128)(2,1)} fusion(bf16[2,2,4,64,1536]{4,3,2,1,0:T(8,128)(2,1)} %get-tuple-element.58, bf16[2,4,2,64,768]{4,3,1,0,2:T(8,128)(2,1)S(1)} %copy-done.19), kind=kOutput, calls=%fused_computation.2 | convolution fusion | flops 2418278400 | bytes 9437184 | tf_op jit(solution)/shard_map/emgcf,mgecd->efd/dot_general | solution.py:30
  331.8 26.3 %reduce-scatter.13.cloned.1.call-done = bf16[1,197,768]{2,1,0:T(8,128)(2,1)} async-done(((bf16[4,197,768]{2,1,0:T(8,128)(2,1)}), bf16[1,197,768]{2,1,0:T(8,128)(2,1)}) %reduce-scatter.13.cloned.1.call-update) | async-done | bytes 302608 | tf_op jit(solution)/shard_map/reduce_scatter | solution.py:158
  364.8 22.8 %reduce-scatter.19.cloned.1.call-done = bf16[192,576]{1,0:T(8,128)(2,1)} async-done(((bf16[768,576]{1,0:T(8,128)(2,1)}), bf16[192,576]{1,0:T(8,128)(2,1)}) %reduce-scatter.19.cloned.1.call-update) | async-done | bytes 221200
  391.8 40.7 %all-reduce = (f32[768]{0:T(1024)}, f32[768]{0:T(1024)}, f32[768,8]{0,1:T(8,128)}) all-reduce(f32[768]{0:T(1024)S(1)} %get-tuple-element.51, f32[768]{0:T(1024)S(1)} %get-tuple-element.49, f32[768,8]{0,1:T(8,128)S(1)} %fusion.91), channel_id=1, replica_groups=mesh['fsdp'=4,'head'=4,'tensor'=2] {'fsdp','head','tensor'}, use_global_device_ids=true, to_apply=%region_23.24 | all-reduce | flops 7680 | bytes 61440 | tf_op jit(solution)/shard_map/psum | solution.py:173
  435.0 13.0 %reduce-scatter.15.cloned.1.call-done = bf16[2,192,1536]{2,1,0:T(8,128)(2,1)} async-done(((bf16[2,768,1536]{2,1,0:T(8,128)(2,1)}), bf16[2,192,1536]{2,1,0:T(8,128)(2,1)}) %reduce-scatter.15.cloned.1.call-update) | async-done | bytes 1179664 | tf_op jit(solution)/shard_map/reduce_scatter | solution.py:166
  450.9 56.8 %reduce-scatter.17.cloned.1.call-done = bf16[2,1536,192]{1,2,0:T(8,128)(2,1)} async-done(((bf16[2,1536,768]{1,2,0:T(8,128)(2,1)}), bf16[2,1536,192]{1,2,0:T(8,128)(2,1)}) %reduce-scatter.17.cloned.1.call-update) | async-done | bytes 1179664 | tf_op jit(solution)/shard_map/reduce_scatter | solution.py:166
  (186 shorter events, 83.4 us)
Async XLA Ops:
  8.0 37.7 %all-gather.5.cloned.1.call-start = ((), (), s32[]{:S(2)}) async-start(), calls=%async_computation.8 | async-start | bytes 1536000 | tf_op jit(solution)/shard_map/all_gather | solution.py:77
  11.7 73.2 %reduce-scatter.11.cloned.1.call-start = ((), (), s32[]{:S(2)}) async-start(), calls=%async_computation.9 | async-start | bytes 1536000 | tf_op jit(solution)/shard_map/reduce_scatter | solution.py:95
  51.2 243.5 %copy-start.2 = (f32[4,3,197,197]{2,3,1,0:T(8,128)}, f32[4,3,197,197]{2,3,1,0:T(8,128)S(1)}, u32[]{:S(2)}) copy-start(f32[4,3,197,197]{2,3,1,0:T(8,128)S(1)} %get-tuple-element.76) | copy-start | bytes 5588500
  55.3 32.0 %copy-start.29 = (f32[768]{0:T(1024)S(1)}, f32[768]{0:T(1024)}, u32[]{:S(2)}) copy-start(f32[768]{0:T(1024)} %param.16) | copy-start | bytes 9220
  55.3 33.1 %copy-start.30 = (bf16[768,8]{0,1:T(8,128)(2,1)S(1)}, bf16[768,8]{0,1:T(8,128)(2,1)}, u32[]{:S(2)}) copy-start(bf16[768,8]{0,1:T(8,128)(2,1)} %param.17) | copy-start | bytes 36868
  55.3 84.6 %all-gather.7.cloned.1.call-start = ((), (), s32[]{:S(2)}) async-start(), calls=%async_computation.10 | async-start | bytes 5898240 | tf_op jit(solution)/shard_map/all_gather | solution.py:78
  55.9 132.4 %all-gather.9.cloned.1.call-start = ((), (), s32[]{:S(2)}) async-start(), calls=%async_computation.11 | async-start | bytes 5898240 | tf_op jit(solution)/shard_map/all_gather | solution.py:79
  132.2 3.8 collective-permute-start
  207.4 3.5 collective-permute-start.1
  212.5 42.0 %all-to-all-start.1 = ((bf16[4,2,64,1536]{3,2,1,0:T(8,128)(2,1)}), bf16[4,2,64,1536]{3,2,1,0:T(8,128)(2,1)}, u32[]{:S(2)}, u32[]{:S(2)}) async-start(bf16[4,2,64,1536]{3,2,1,0:T(8,128)(2,1)} %copy.114), calls=%async_computation.2 | async-start | bytes 3145728 | tf_op jit(solution)/shard_map/all_to_all | solution.py:131
  217.1 74.2 %all-gather.11.cloned.1.call-start = ((), (), s32[]{:S(2)}) async-start(), calls=%async_computation.12 | async-start | bytes 1536000 | tf_op jit(solution)/shard_map/all_gather | solution.py:145
  258.4 32.9 %copy-start.17 = (bf16[192,768]{0,1:T(8,128)(2,1)S(1)}, bf16[192,768]{0,1:T(8,128)(2,1)}, u32[]{:S(2)}) copy-start(bf16[192,768]{0,1:T(8,128)(2,1)} %all_gather.20) | copy-start | bytes 884740
  261.9 68.7 %reduce-scatter.21.cloned.1.call-start = ((), (), s32[]{:S(2)}) async-start(), calls=%async_computation.17 | async-start | bytes 491520
  300.9 57.1 %reduce-scatter.13.cloned.1.call-start = ((), (), s32[]{:S(2)}) async-start(), calls=%async_computation.13 | async-start | bytes 1536000 | tf_op jit(solution)/shard_map/reduce_scatter | solution.py:158
  306.8 80.8 %reduce-scatter.19.cloned.1.call-start = ((), (), s32[]{:S(2)}) async-start(), calls=%async_computation.16 | async-start | bytes 1228800
  313.0 135.0 %reduce-scatter.15.cloned.1.call-start = ((), (), s32[]{:S(2)}) async-start(), calls=%async_computation.14 | async-start | bytes 5898240 | tf_op jit(solution)/shard_map/reduce_scatter | solution.py:166
  320.2 187.5 %reduce-scatter.17.cloned.1.call-start = ((), (), s32[]{:S(2)}) async-start(), calls=%async_computation.15 | async-start | bytes 5898240 | tf_op jit(solution)/shard_map/reduce_scatter | solution.py:166
  327.9 32.8 %copy-start.5 = (bf16[1,1,197,768]{3,0,2,1:T(2,128)(2,1)S(1)}, bf16[1,1,197,768]{3,0,2,1:T(2,128)(2,1)}, u32[]{:S(2)}) copy-start(bf16[1,1,197,768]{3,0,2,1:T(2,128)(2,1)} %copy-done.3) | copy-start | bytes 907780
  327.9 32.8 %copy-start.10 = (f32[1,197,768]{2,1,0:T(8,128)S(1)}, f32[1,197,768]{2,1,0:T(8,128)}, u32[]{:S(2)}) copy-start(f32[1,197,768]{2,1,0:T(8,128)} %copy-done.9) | copy-start | bytes 1815556
  328.9 1.6 collective-permute-start.2
  331.6 57.5 %collective-permute-start.5 = (bf16[192,192]{1,0:T(8,128)(2,1)S(1)}, bf16[192,192]{1,0:T(8,128)(2,1)S(1)}, u32[]{:S(2)}, u32[]{:S(2)}) collective-permute-start(bf16[192,192]{1,0:T(8,128)(2,1)S(1)} %copy.150), channel_id=1, source_target_pairs={{0,1},{1,0},{2,3},{3,2},{4,5},{5,4},{6,7},{7,6},{8,9},{9,8},{10,11... | collective-permute-start | bytes 221192 | tf_op jit(solution)/shard_map/ppermute | solution.py:34
  363.4 69.0 %collective-permute-start.3 = (f32[1,197,768]{2,0,1:T(1,128)}, f32[1,197,768]{2,0,1:T(1,128)S(1)}, u32[]{:S(2)}, u32[]{:S(2)}) collective-permute-start(f32[1,197,768]{2,0,1:T(1,128)} %copy.123), channel_id=1, source_target_pairs={{0,1},{1,0},{2,3},{3,2},{4,5},{5,4},{6,7},{7,6},{8,9},{9,8},{10,11... | collective-permute-start | bytes 1815560 | tf_op jit(solution)/shard_map/ppermute | solution.py:34
  389.0 1.6 collective-permute-start.4
  432.7 78.0 %copy-start.1 = (bf16[2,1,197,768]{3,0,2,1:T(2,128)(2,1)S(1)}, bf16[2,1,197,768]{3,0,2,1:T(2,128)(2,1)}, u32[]{:S(2)}) copy-start(bf16[2,1,197,768]{3,0,2,1:T(2,128)(2,1)} %param.12) | copy-start | bytes 1815556
  (29 other events, 143.6 us)
Sparse Core Ops, SparseCore 0:
  11.9 33.8 all-gather.4
  55.4 29.4 reduce-scatter.10
  262.0 29.2 all-gather.10
Sparse Core Ops, SparseCore 1:
  57.7 56.0 all-gather.6
  132.3 55.9 all-gather.8
  301.0 23.8 reduce-scatter.20
  327.8 30.2 reduce-scatter.12
  361.6 25.9 reduce-scatter.18
  390.6 57.3 reduce-scatter.14
  450.8 56.8 reduce-scatter.16
where the time goes:
time: 525 us; the launch traced here: 518 us
  waiting for transfers between devices  247 us (47%)
  blocking collectives  110 us (21%)
  matrix products  65.6 us (12%)
  other arithmetic  44.1 us (8%)
  local copies, waits for them, and re-layouts  28.8 us (5%)
  between operations  16.2 us (3%)
  starting transfers between devices  5.72 us (1%)
    reduce_scatter x2, waiting for transfers between devices, owner(): lax.psum_scatter(part.astype(bf16), 'fsdp', scatter_dimension=dim, tiled=...  69.8 us
    dot_general x19, matrix products, ein(): return jnp.einsum(spec, left, right, preferred_element_type=f32)  62.4 us
    psum x1, blocking collectives, on_device(): lax.psum((grad_gain_one, grad_gain_two, grad_router), ('fsdp', 'head', 't...  40.7 us
    all_to_all x1, blocking collectives, on_device(): mine = lax.all_to_all(sent, 'head', split_axis=0, concat_axis=0, tiled=True)  39.7 us
    all_to_all x1, waiting for transfers between devices, on_device(): back = lax.all_to_all(back, 'head', split_axis=0, concat_axis=0, tiled=True)  37.2 us
    all_gather x1, waiting for transfers between devices, on_device(): lax.all_gather(hidden_grad.astype(bf16), 'head', axis=0, tiled=True)  29.3 us
    reduce_scatter x1, waiting for transfers between devices, on_device(): lax.psum_scatter(row_part.astype(bf16), 'head', scatter_dimension=0, tile...  26.3 us
    reduce_scatter x1, waiting for transfers between devices, on_device(): lax.psum_scatter(partial_att.astype(bf16), 'head', scatter_dimension=0, t...  25.5 us
  transfers between devices with their start and end apart: 17, of which 13 were waited for; matrix products, arithmetic and copies ran while one was open for 15% of the time, Pallas kernels for 0%

commit v1 on v0

--- a/solution.py
+++ b/solution.py
@@ -2,6 +2,7 @@
 import jax.numpy as jnp
 from jax import lax
 from jax.sharding import PartitionSpec as P
+from jax.lax import axis_index, axis_size, ppermute
 
 HD = 64
 TOP = 2
@@ -10,6 +11,31 @@
 norm_eps = 1e-06
 f32 = jnp.float32
 bf16 = jnp.bfloat16
+
+
+def _expand_body(named_axis, local_array):
+    f_next = axis_size(named_axis)
+    wide_out, found_now, z1 = (f_next, axis_index(named_axis), local_array.shape[2])
+    r1 = tuple(
+        (hop_no * wide_out if dd == 2 else hop_no for dd, hop_no in enumerate(local_array.shape))
+    )
+    carry = jnp.zeros(r1, local_array.dtype)
+    local_part = lax.dynamic_update_slice_in_dim(carry, local_array, found_now * z1, axis=2)
+    response = clean = local_array
+    for j in range(1, wide_out // 2 + 1):
+        response = ppermute(
+            response, named_axis, tuple(((dd, (dd + 1) % wide_out) for dd in range(wide_out)))
+        )
+        local_part = lax.dynamic_update_slice_in_dim(
+            local_part, response, (found_now - j) % wide_out * z1, axis=2
+        )
+        if 2 * j < wide_out:
+            m_next = tuple(((dd, (dd - 1) % wide_out) for dd in range(wide_out)))
+            clean = ppermute(clean, named_axis, m_next)
+            local_part = lax.dynamic_update_slice_in_dim(
+                local_part, clean, (found_now + j) % wide_out * z1, axis=2
+            )
+    return local_part
 
 
 def norm_rows(values, gain_vec):
@@ -76,7 +102,7 @@
     normed, norm_back_one = jax.vjp(norm_rows, inputs, gain_one)
     rows_all = lax.all_gather(normed.astype(bf16), "head", axis=0, tiled=True)
     in_full = lax.all_gather(w_in, "fsdp", axis=1, tiled=True)
-    down_full = lax.all_gather(w_down, "fsdp", axis=2, tiled=True)
+    down_full = _expand_body("fsdp", w_down)
     image_total = rows_all.shape[0]
     head_shape = (image_total, seq_length, local_heads, HD)
     project = ein("bsd,pde->pbse", rows_all, qkv_full)

time: 525 us -> 580 us (1.10)
  local copies, waits for them, and re-layouts: 28.8 us -> 104 us
  blocking collectives: 110 us -> 70.3 us
  waiting for transfers between devices: 247 us -> 258 us
  starting transfers between devices: 5.72 us -> 14.8 us
    dynamic_update_slice x0 -> x4, local copies, waits for them, and re-layouts: none -> 64.5 us  [the longest x2 31.8 us: _expand_body(): lax.dynamic_update_slice_in_dim(local_part, response, (found_now - j) % w...]
    all_to_all x1 -> x0, blocking collectives: 39.7 us -> none  [on_device(): mine = lax.all_to_all(sent, 'head', split_axis=0, concat_axis=0, tiled=True)]
    all_to_all x0 -> x1, waiting for transfers between devices: none -> 35.4 us  [on_device(): mine = lax.all_to_all(sent, 'head', split_axis=0, concat_axis=0, tiled=True)]
    all_gather x1 -> x0, waiting for transfers between devices: 23.6 us -> none  [on_device(): down_full = lax.all_gather(w_down, 'fsdp', axis=2, tiled=True)]
    ppermute x0 -> x3, local copies, waits for them, and re-layouts: none -> 7.51 us  [the longest x2 5.01 us: _expand_body(): ppermute(response, named_axis, tuple(((dd, (dd + 1) % wide_out) for dd in...]
    unnamed x12 -> x11, waiting for transfers between devices: 23.5 us -> 24.2 us
    unnamed x83 -> x80, local copies, waits for them, and re-layouts: 20.7 us -> 20.6 us
  transfers between devices with their start and end apart: 17 -> 20, of which waited for: 13 -> 12; matrix products, arithmetic and copies ran while one was open for 15% -> 24% of each run, Pallas kernels for 0% -> 0%
where the time goes in v1:
time: 580 us; the launch traced here: 571 us
  waiting for transfers between devices  258 us (44%)
  local copies, waits for them, and re-layouts  104 us (18%)
  blocking collectives  70.3 us (12%)
  matrix products  62.9 us (11%)
  other arithmetic  44.5 us (8%)
  between operations  16.3 us (3%)
  starting transfers between devices  14.8 us (3%)
    reduce_scatter x2, waiting for transfers between devices, owner(): lax.psum_scatter(part.astype(bf16), 'fsdp', scatter_dimension=dim, tiled=...  69.8 us
    dot_general x19, matrix products, ein(): return jnp.einsum(spec, left, right, preferred_element_type=f32)  59.8 us
    psum x1, blocking collectives, on_device(): lax.psum((grad_gain_one, grad_gain_two, grad_router), ('fsdp', 'head', 't...  40.7 us
    all_to_all x1, waiting for transfers between devices, on_device(): back = lax.all_to_all(back, 'head', split_axis=0, concat_axis=0, tiled=True)  37.4 us
    all_to_all x1, waiting for transfers between devices, on_device(): mine = lax.all_to_all(sent, 'head', split_axis=0, concat_axis=0, tiled=True)  35.4 us
    dynamic_update_slice x2, local copies, waits for them, and re-layouts, _expand_body(): lax.dynamic_update_slice_in_dim(local_part, response, (found_now - j) % w...  31.8 us
    all_gather x1, waiting for transfers between devices, on_device(): lax.all_gather(hidden_grad.astype(bf16), 'head', axis=0, tiled=True)  30.7 us
    reduce_scatter x1, waiting for transfers between devices, on_device(): lax.psum_scatter(partial_att.astype(bf16), 'head', scatter_dimension=0, t...  26.3 us
  transfers between devices with their start and end apart: 20, of which 12 were waited for; matrix products, arithmetic and copies ran while one was open for 24% of the time, Pallas kernels for 0%

profile of v1, /device:TPU:0, one launch (start us, length us, event | category | flops | bytes accessed | tf_op | source)
XLA Modules:
  0.0 570.7 jit_solution(12804070901484625287)
XLA Ops:
  12.2 19.2 %all_gather.16 = bf16[3,768,192]{2,0,1:T(4,128)(2,1)S(1)} all-gather(bf16[3,192,192]{2,0,1:T(4,128)(2,1)S(1)} %copy.117), channel_id=1, replica_groups=mesh['fsdp'=4,'head'=4,'tensor'=2] {'fsdp'}, dimensions={1}, use_global_device_ids=true | all-gather | bytes 1105920 | tf_op jit(solution)/shard_map/all_gather | solution.py:95
  32.3 10.4 %all_gather.17 = bf16[192,768]{0,1:T(8,128)(2,1)} all-gather(bf16[192,192]{0,1:T(8,128)(2,1)S(1)} %copy.120), channel_id=1, replica_groups=mesh['fsdp'=4,'head'=4,'tensor'=2] {'fsdp'}, dimensions={1}, use_global_device_ids=true | all-gather | bytes 368640 | tf_op jit(solution)/shard_map/all_gather | solution.py:96
  58.8 26.3 %reduce-scatter.11.cloned.1.call-done = bf16[1,197,768]{2,1,0:T(8,128)(2,1)} async-done(((bf16[4,197,768]{2,1,0:T(8,128)(2,1)}), bf16[1,197,768]{2,1,0:T(8,128)(2,1)}) %reduce-scatter.11.cloned.1.call-update) | async-done | bytes 302608 | tf_op jit(solution)/shard_map/reduce_scatter | solution.py:121
  92.6 4.4 all-to-all-start
  98.5 35.4 %all-to-all-done = bf16[4,2,64,1536]{3,2,1,0:T(8,128)(2,1)} async-done(((bf16[4,2,64,1536]{3,2,1,0:T(8,128)(2,1)}), bf16[4,2,64,1536]{3,2,1,0:T(8,128)(2,1)}, u32[]{:S(2)}, u32[]{:S(2)}) %all-to-all-start) | async-done | bytes 1572896 | tf_op jit(solution)/shard_map/all_to_all | solution.py:142
  145.5 15.3 %dynamic_update_slice.12 = bf16[2,1536,768]{2,1,0:T(8,128)(2,1)} dynamic-update-slice(bf16[2,1536,768]{2,1,0:T(8,128)(2,1)} %broadcast_in_dim.16, bf16[2,1536,192]{2,1,0:T(8,128)(2,1)} %copy.122, s32[]{:T(128)} %constant.50.clone.1, s32[]{:T(128)} %constant.50.clone.1, s32[]{:T(128)S(6)} %select_n.60) | dynamic-update-slice | bytes 2359300 | tf_op jit(solution)/shard_map/dynamic_update_slice | solution.py:23
  163.3 16.7 %dynamic_update_slice.13 = bf16[2,1536,768]{2,1,0:T(8,128)(2,1)} dynamic-update-slice(bf16[2,1536,768]{2,1,0:T(8,128)(2,1)} %dynamic_update_slice.12, bf16[2,1536,192]{2,1,0:T(8,128)(2,1)} %copy.123, s32[]{:T(128)} %constant.50.clone.1, s32[]{:T(128)} %constant.50.clone.1, s32[]{:T(128)S(6)} %select_n.62) | dynamic-update-slice | bytes 2359300 | tf_op jit(solution)/shard_map/dynamic_update_slice | solution.py:29
  182.5 17.4 %dynamic_update_slice.14 = bf16[2,1536,768]{2,1,0:T(8,128)(2,1)} dynamic-update-slice(bf16[2,1536,768]{2,1,0:T(8,128)(2,1)} %dynamic_update_slice.13, bf16[2,1536,192]{2,1,0:T(8,128)(2,1)} %copy.124, s32[]{:T(128)} %constant.50.clone.1, s32[]{:T(128)} %constant.50.clone.1, s32[]{:T(128)S(6)} %select_n.64) | dynamic-update-slice | bytes 2359300 | tf_op jit(solution)/shard_map/dynamic_update_slice | solution.py:35
  202.4 15.1 %dynamic_update_slice.15 = bf16[2,1536,768]{2,1,0:T(8,128)(2,1)} dynamic-update-slice(bf16[2,1536,768]{2,1,0:T(8,128)(2,1)} %dynamic_update_slice.14, bf16[2,1536,192]{2,1,0:T(8,128)(2,1)} %copy.125, s32[]{:T(128)} %constant.50.clone.1, s32[]{:T(128)} %constant.50.clone.1, s32[]{:T(128)S(6)} %select_n.66) | dynamic-update-slice | bytes 2359300 | tf_op jit(solution)/shard_map/dynamic_update_slice | solution.py:29
  217.6 3.9 pad_maximum_fusion.1
  221.4 6.6 %fusion.33 = (u8[2,2,64,1536]{3,2,1,0:T(8,128)(4,1)S(1)}, u8[2,2,64,1536]{3,2,1,0:T(8,128)(4,1)S(1)}, f32[2,2,4,64,1536]{4,3,2,1,0:T(8,128)S(1)}) fusion(bf16[2,4,2,64,768]{4,3,1,0,2:T(8,128)(2,1)} %get-tuple-element.63, bf16[2,768,1536]{2,1,0:T(8,128)(2,1)} %all-gather.6.cloned.1.call-done), kind=kOutput, calls=%fused_computation.59 | convolution fusion | flops 2435579904 | bytes 13369344 | tf_op jit(solution)/shard_map/mgecd,edf->emgcf/dot_general | solution.py:56
  228.1 15.1 %multiply_convert_fusion = (bf16[2,2,4,64,1536]{4,3,2,1,0:T(8,128)(2,1)S(1)}, f32[2,2,4,64,1536]{4,3,2,1,0:T(8,128)}) fusion(f32[2,2,4,64,1536]{4,3,2,1,0:T(8,128)S(1)} %get-tuple-element.79, u8[2,2,64,1536]{3,2,1,0:T(8,128)(4,1)S(1)} %get-tuple-element.46, u8[2,2,64,1536]{3,2,1,0:T(8,128)(4,1)S(1)} %get-tuple-element.45), kind=kLoop, calls=%fused_computation.13 | loop fusion | flops 110100480 | bytes 16515072 | tf_op jit(solution)/shard_map/convert_element_type | solution.py:148
  245.8 8.6 %add_convert_fusion = bf16[2,2,4,64,1536]{4,3,2,1,0:T(8,128)(2,1)} fusion(f32[2,2,4,64,1536]{4,3,2,1,0:T(8,128)} %get-tuple-element.59, bf16[2,4,2,64,768]{4,3,1,0,2:T(8,128)(2,1)S(1)} %copy-done.16, f32[2,2,4,64,1536]{4,3,2,1,0:T(8,128)S(1)} %get-tuple-element.79, bf16[2,1536,768]{2,1,0:T(8,128)(2,1)} %dynamic_update_slice.15), kind=kOutput, calls=%fused_computation.12 | convolution fusion | flops 2437939200 | bytes 22020096 | tf_op jit(solution)/shard_map/mgecd,efd->emgcf/dot_general | solution.py:56
  254.4 5.9 %fusion.25 = f32[2,4,2,64,768]{4,3,1,0,2:T(8,128)S(1)} fusion(bf16[2,2,4,64,1536]{4,3,2,1,0:T(8,128)(2,1)} %add_convert_fusion, bf16[2,768,1536]{2,1,0:T(8,128)(2,1)} %all-gather.6.cloned.1.call-done), kind=kOutput, calls=%fused_computation.50 | convolution fusion | flops 2415919104 | bytes 11010048 | tf_op jit(solution)/shard_map/emgcf,edf->mgecd/dot_general | solution.py:56
  265.7 5.2 all-to-all-start.1
  270.9 37.4 %all-to-all-done.1 = bf16[4,2,64,1536]{3,2,1,0:T(8,128)(2,1)} async-done(((bf16[4,2,64,1536]{3,2,1,0:T(8,128)(2,1)}), bf16[4,2,64,1536]{3,2,1,0:T(8,128)(2,1)}, u32[]{:S(2)}, u32[]{:S(2)}) %all-to-all-start.1) | async-done | bytes 1572896 | tf_op jit(solution)/shard_map/all_to_all | solution.py:157
  314.5 30.7 %all-gather.8.cloned.1.call-done = bf16[4,197,768]{2,1,0:T(8,128)(2,1)} async-done(((bf16[1,197,768]{2,1,0:T(8,128)(2,1)}), bf16[4,197,768]{2,1,0:T(8,128)(2,1)}) %all-gather.8.cloned.1.call-update) | async-done | bytes 1210384 | tf_op jit(solution)/shard_map/all_gather | solution.py:171
  366.4 7.2 %bitcast_convert_fusion.1 = bf16[2,768,1536]{2,1,0:T(8,128)(2,1)} fusion(bf16[2,2,4,64,1536]{4,3,2,1,0:T(8,128)(2,1)} %add_convert_fusion, bf16[2,4,2,64,768]{4,3,1,0,2:T(8,128)(2,1)} %get-tuple-element.63), kind=kOutput, calls=%fused_computation.3 | convolution fusion | flops 2418278400 | bytes 9437184 | tf_op jit(solution)/shard_map/mgecd,emgcf->edf/dot_general | solution.py:56
  375.0 6.3 %bitcast_convert_fusion = bf16[2,1536,768]{1,2,0:T(8,128)(2,1)} fusion(bf16[2,2,4,64,1536]{4,3,2,1,0:T(8,128)(2,1)} %copy-done.15, bf16[2,4,2,64,768]{4,3,1,0,2:T(8,128)(2,1)S(1)} %copy-done.17), kind=kOutput, calls=%fused_computation.2 | convolution fusion | flops 2418278400 | bytes 9437184 | tf_op jit(solution)/shard_map/emgcf,mgecd->efd/dot_general | solution.py:56
  385.1 25.5 %reduce-scatter.13.cloned.1.call-done = bf16[1,197,768]{2,1,0:T(8,128)(2,1)} async-done(((bf16[4,197,768]{2,1,0:T(8,128)(2,1)}), bf16[1,197,768]{2,1,0:T(8,128)(2,1)}) %reduce-scatter.13.cloned.1.call-update) | async-done | bytes 302608 | tf_op jit(solution)/shard_map/reduce_scatter | solution.py:184
  416.6 23.5 %reduce-scatter.19.cloned.1.call-done = bf16[192,576]{1,0:T(8,128)(2,1)} async-done(((bf16[768,576]{1,0:T(8,128)(2,1)}), bf16[192,576]{1,0:T(8,128)(2,1)}) %reduce-scatter.19.cloned.1.call-update) | async-done | bytes 221200
  444.4 40.7 %all-reduce = (f32[768]{0:T(1024)}, f32[768]{0:T(1024)}, f32[768,8]{0,1:T(8,128)}) all-reduce(f32[768]{0:T(1024)S(1)} %get-tuple-element.51, f32[768]{0:T(1024)S(1)} %get-tuple-element.49, f32[768,8]{0,1:T(8,128)S(1)} %fusion.91), channel_id=1, replica_groups=mesh['fsdp'=4,'head'=4,'tensor'=2] {'fsdp','head','tensor'}, use_global_device_ids=true, to_apply=%region_23.24 | all-reduce | flops 7680 | bytes 61440 | tf_op jit(solution)/shard_map/psum | solution.py:199
  487.6 12.9 %reduce-scatter.15.cloned.1.call-done = bf16[2,192,1536]{2,1,0:T(8,128)(2,1)} async-done(((bf16[2,768,1536]{2,1,0:T(8,128)(2,1)}), bf16[2,192,1536]{2,1,0:T(8,128)(2,1)}) %reduce-scatter.15.cloned.1.call-update) | async-done | bytes 1179664 | tf_op jit(solution)/shard_map/reduce_scatter | solution.py:192
  503.4 56.9 %reduce-scatter.17.cloned.1.call-done = bf16[2,1536,192]{1,2,0:T(8,128)(2,1)} async-done(((bf16[2,1536,768]{1,2,0:T(8,128)(2,1)}), bf16[2,1536,192]{1,2,0:T(8,128)(2,1)}) %reduce-scatter.17.cloned.1.call-update) | async-done | bytes 1179664 | tf_op jit(solution)/shard_map/reduce_scatter | solution.py:192
  (195 shorter events, 108.0 us)
Async XLA Ops:
  8.0 37.7 %all-gather.4.cloned.1.call-start = ((), (), s32[]{:S(2)}) async-start(), calls=%async_computation.8 | async-start | bytes 1536000 | tf_op jit(solution)/shard_map/all_gather | solution.py:103
  11.7 73.4 %reduce-scatter.11.cloned.1.call-start = ((), (), s32[]{:S(2)}) async-start(), calls=%async_computation.9 | async-start | bytes 1536000 | tf_op jit(solution)/shard_map/reduce_scatter | solution.py:121
  55.5 32.0 %copy-start.28 = (f32[768]{0:T(1024)S(1)}, f32[768]{0:T(1024)}, u32[]{:S(2)}) copy-start(f32[768]{0:T(1024)} %param.16) | copy-start | bytes 9220
  55.5 33.1 %copy-start.29 = (bf16[768,8]{0,1:T(8,128)(2,1)S(1)}, bf16[768,8]{0,1:T(8,128)(2,1)}, u32[]{:S(2)}) copy-start(bf16[768,8]{0,1:T(8,128)(2,1)} %param.17) | copy-start | bytes 36868
  55.6 165.9 %all-gather.6.cloned.1.call-start = ((), (), s32[]{:S(2)}) async-start(), calls=%async_computation.10 | async-start | bytes 5898240 | tf_op jit(solution)/shard_map/all_gather | solution.py:104
  92.6 41.3 %all-to-all-start = ((bf16[4,2,64,1536]{3,2,1,0:T(8,128)(2,1)}), bf16[4,2,64,1536]{3,2,1,0:T(8,128)(2,1)}, u32[]{:S(2)}, u32[]{:S(2)}) async-start(bf16[4,2,64,1536]{3,2,1,0:T(8,128)(2,1)} %bitcast.259), calls=%async_computation.1 | async-start | bytes 3145728 | tf_op jit(solution)/shard_map/all_to_all | solution.py:142
  96.9 43.0 %collective-permute-start = (bf16[2,1536,192]{1,2,0:T(8,128)(2,1)}, bf16[2,1536,192]{1,2,0:T(8,128)(2,1)}, u32[]{:S(2)}, u32[]{:S(2)}) collective-permute-start(bf16[2,1536,192]{1,2,0:T(8,128)(2,1)} %param.19), channel_id=1, source_target_pairs={{0,8},{8,16},{16,24},{24,0},{1,9},{9,17},{17,25},{25,1},{2,10},{10... | collective-permute-start | bytes 3538952 | tf_op jit(solution)/shard_map/ppermute | solution.py:26
  136.5 81.1 %collective-permute-start.3 = (bf16[4,2,64,1536]{3,2,0,1:T(8,128)(2,1)}, bf16[4,2,64,1536]{3,2,0,1:T(8,128)(2,1)}, u32[]{:S(2)}, u32[]{:S(2)}) collective-permute-start(bf16[4,2,64,1536]{3,2,0,1:T(8,128)(2,1)} %copy.190), channel_id=1, source_target_pairs={{0,1},{1,0},{2,3},{3,2},{4,5},{5,4},{6,7},{7,6},{8,9},{9,8},{10,11... | collective-permute-start | bytes 4718600 | tf_op jit(solution)/shard_map/ppermute | solution.py:60
  136.5 43.5 %collective-permute-start.1 = (bf16[2,1536,192]{1,2,0:T(8,128)(2,1)}, bf16[2,1536,192]{1,2,0:T(8,128)(2,1)}, u32[]{:S(2)}, u32[]{:S(2)}) collective-permute-start(bf16[2,1536,192]{1,2,0:T(8,128)(2,1)} %param.19), channel_id=1, source_target_pairs={{0,24},{8,0},{16,8},{24,16},{1,25},{9,1},{17,9},{25,17},{2,26},{10... | collective-permute-start | bytes 3538952 | tf_op jit(solution)/shard_map/ppermute | solution.py:34
  139.9 59.9 %collective-permute-start.2 = (bf16[2,1536,192]{1,2,0:T(8,128)(2,1)}, bf16[2,1536,192]{1,2,0:T(8,128)(2,1)}, u32[]{:S(2)}, u32[]{:S(2)}) collective-permute-start(bf16[2,1536,192]{1,2,0:T(8,128)(2,1)} %collective-permute-done), channel_id=1, source_target_pairs={{0,8},{8,16},{16,24},{24,0},{1,9},{9,17},{17,25},{25,1},{2,10},{10... | collective-permute-start | bytes 3538952 | tf_op jit(solution)/shard_map/ppermute | solution.py:26
  260.5 3.5 collective-permute-start.4
  265.7 42.5 %all-to-all-start.1 = ((bf16[4,2,64,1536]{3,2,1,0:T(8,128)(2,1)}), bf16[4,2,64,1536]{3,2,1,0:T(8,128)(2,1)}, u32[]{:S(2)}, u32[]{:S(2)}) async-start(bf16[4,2,64,1536]{3,2,1,0:T(8,128)(2,1)} %copy.130), calls=%async_computation.2 | async-start | bytes 3145728 | tf_op jit(solution)/shard_map/all_to_all | solution.py:157
  270.8 74.4 %all-gather.8.cloned.1.call-start = ((), (), s32[]{:S(2)}) async-start(), calls=%async_computation.11 | async-start | bytes 1536000 | tf_op jit(solution)/shard_map/all_gather | solution.py:171
  314.5 69.5 %reduce-scatter.21.cloned.1.call-start = ((), (), s32[]{:S(2)}) async-start(), calls=%async_computation.16 | async-start | bytes 491520
  353.6 57.0 %reduce-scatter.13.cloned.1.call-start = ((), (), s32[]{:S(2)}) async-start(), calls=%async_computation.12 | async-start | bytes 1536000 | tf_op jit(solution)/shard_map/reduce_scatter | solution.py:184
  359.9 80.2 %reduce-scatter.19.cloned.1.call-start = ((), (), s32[]{:S(2)}) async-start(), calls=%async_computation.15 | async-start | bytes 1228800
  366.2 134.3 %reduce-scatter.15.cloned.1.call-start = ((), (), s32[]{:S(2)}) async-start(), calls=%async_computation.13 | async-start | bytes 5898240 | tf_op jit(solution)/shard_map/reduce_scatter | solution.py:192
  373.6 186.8 %reduce-scatter.17.cloned.1.call-start = ((), (), s32[]{:S(2)}) async-start(), calls=%async_computation.14 | async-start | bytes 5898240 | tf_op jit(solution)/shard_map/reduce_scatter | solution.py:192
  381.3 32.0 %copy-start.6 = (f32[1,197,768]{2,1,0:T(8,128)S(1)}, f32[1,197,768]{2,1,0:T(8,128)}, u32[]{:S(2)}) copy-start(f32[1,197,768]{2,1,0:T(8,128)} %copy-done.5) | copy-start | bytes 1815556
  382.3 1.6 collective-permute-start.5
  384.9 56.7 %collective-permute-start.8 = (bf16[192,192]{1,0:T(8,128)(2,1)S(1)}, bf16[192,192]{1,0:T(8,128)(2,1)}, u32[]{:S(2)}, u32[]{:S(2)}) collective-permute-start(bf16[192,192]{1,0:T(8,128)(2,1)S(1)} %copy.166), channel_id=1, source_target_pairs={{0,1},{1,0},{2,3},{3,2},{4,5},{5,4},{6,7},{7,6},{8,9},{9,8},{10,11... | collective-permute-start | bytes 221192 | tf_op jit(solution)/shard_map/ppermute | solution.py:60
  415.2 69.9 %collective-permute-start.6 = (f32[1,197,768]{2,0,1:T(1,128)S(1)}, f32[1,197,768]{2,0,1:T(1,128)S(1)}, u32[]{:S(2)}, u32[]{:S(2)}) collective-permute-start(f32[1,197,768]{2,0,1:T(1,128)S(1)} %copy.139), channel_id=1, source_target_pairs={{0,1},{1,0},{2,3},{3,2},{4,5},{5,4},{6,7},{7,6},{8,9},{9,8},{10,11... | collective-permute-start | bytes 1815560 | tf_op jit(solution)/shard_map/ppermute | solution.py:60
  441.5 1.7 collective-permute-start.7
  485.3 78.0 %copy-start.1 = (bf16[2,1,197,768]{3,0,2,1:T(2,128)(2,1)S(1)}, bf16[2,1,197,768]{3,0,2,1:T(2,128)(2,1)}, u32[]{:S(2)}) copy-start(bf16[2,1,197,768]{3,0,2,1:T(2,128)(2,1)} %param.12) | copy-start | bytes 1815556
  (30 other events, 122.0 us)
Sparse Core Ops, SparseCore 0:
  11.9 33.8 all-gather.3
  55.7 29.4 reduce-scatter.10
  314.6 30.5 all-gather.7
Sparse Core Ops, SparseCore 1:
  57.9 69.3 all-gather.5
  353.7 23.8 reduce-scatter.20
  380.4 30.2 reduce-scatter.12
  414.2 25.9 reduce-scatter.18
  443.2 57.3 reduce-scatter.14
  503.5 56.8 reduce-scatter.16
